TPU v7x, 32 devices: a whole 2x2x4 slice. The times are simulated.
32 devices in a mesh: tm: 4 (over y, x), slab: 8 (over z, core).
Axes of the slice: x: 2, y: 2, z: 4, core: 2. Of those that a mesh axis runs over, the one named last changes fastest.
Arguments:
- velocity: bfloat16 [4, 3, 2, 131072], P('tm', None, None, 'slab'), may hold values from -64 to 64
- shell_index: int32 [131072], P('slab'), may hold values from 0 to 127, as said below
- ref_order: int32 [4], replicated, may hold values from 0 to 3, each once
Outputs:
- coherence: float32 [4, 4, 128], P('tm')
- spectrum: float32 [4, 128], P('tm')
Inputs may be any that keep to these rules, and one draw needn't show every extreme that they name: `shell_index`: every shell number from 0 to 127 is taken by some mode. `ref_order`: each snapshot number appears once.
All inputs are finite; a program needn't handle non-finite values.
Results may differ from a plain program's by a relative error of at most 0.0003.
Values may be sent and summed in bfloat16 or wider, within the bound.
A program may use at most 64 MiB of HBM per device.

v0:
```python
import math

import jax
import jax.numpy as jnp
from jax import lax
from jax.sharding import PartitionSpec as P

SHELLS = 128


def bin_modes(cross_terms, energy_terms, shell_ids):
    mode_count = cross_terms.shape[1]
    block_size = math.gcd(mode_count, 4096)
    columns = jnp.arange(SHELLS, dtype=jnp.int32)

    def add_block(step_index, totals):
        first_row = step_index * block_size
        block_ids = lax.dynamic_slice_in_dim(shell_ids, first_row, block_size, 0)
        onehot = (block_ids[:, None] == columns[None, :]).astype(jnp.bfloat16)
        cross_block = lax.dynamic_slice_in_dim(cross_terms, first_row, block_size, 1)
        energy_block = lax.dynamic_slice_in_dim(energy_terms, first_row, block_size, 1)
        return (
            totals[0] + jnp.dot(cross_block, onehot, preferred_element_type=jnp.float32),
            totals[1] + jnp.dot(energy_block, onehot, preferred_element_type=jnp.float32),
        )

    initial = (
        jnp.zeros((cross_terms.shape[0], SHELLS), jnp.float32),
        jnp.zeros((energy_terms.shape[0], SHELLS), jnp.float32),
    )
    return lax.fori_loop(0, mode_count // block_size, add_block, initial)


def pair_terms(own_field, ref_modes):
    own_wide = own_field.astype(jnp.float32)
    ref_wide = ref_modes.astype(jnp.float32)
    real_part = jnp.sum(own_wide * ref_wide, axis=(0, 1))
    imag_part = jnp.sum(own_wide[:, 1] * ref_wide[:, 0] - own_wide[:, 0] * ref_wide[:, 1], axis=0)
    return jnp.stack([real_part, imag_part], axis=0).astype(jnp.bfloat16)


def body(velocity, shell_index, ref_order):
    snapshots = lax.axis_size("tm")
    mode_count = velocity.shape[3]
    own_field = velocity[0]
    empty_rows = jnp.zeros((snapshots, 2, mode_count), jnp.bfloat16)
    pieces = lax.all_gather(velocity, "tm", axis=0, tiled=True)

    def place_one(offset, buffer):
        ref_modes = lax.dynamic_index_in_dim(pieces, offset, 0, keepdims=False)
        return lax.dynamic_update_slice_in_dim(
            buffer, pair_terms(own_field, ref_modes)[None], offset, 0
        )

    cross_rows = lax.fori_loop(0, pieces.shape[0], place_one, empty_rows)
    own_wide = own_field.astype(jnp.float32)
    energy_terms = jnp.sum(own_wide * own_wide, axis=(0, 1)).astype(jnp.bfloat16)[None]
    partial_cross, partial_energy = bin_modes(
        cross_rows.reshape(snapshots * 2, mode_count), energy_terms, shell_index
    )
    total_cross, own_spectrum = lax.psum((partial_cross, partial_energy), "slab")
    all_spectra = lax.all_gather(own_spectrum, "tm", axis=0, tiled=True)
    order_hot = (ref_order[:, None] == jnp.arange(snapshots, dtype=jnp.int32)[None, :]).astype(
        jnp.float32
    )
    chosen = jnp.einsum(
        "js,spk->jpk",
        order_hot,
        total_cross.reshape(snapshots, 2, SHELLS),
        precision=lax.Precision.HIGHEST,
    )
    ref_energy = jnp.dot(
        order_hot, all_spectra, precision=lax.Precision.HIGHEST, preferred_element_type=jnp.float32
    )
    power_sum = chosen[:, 0] * chosen[:, 0] + chosen[:, 1] * chosen[:, 1]
    coherence = power_sum / (own_spectrum * ref_energy)
    return (coherence[None], own_spectrum)


def solution(mesh):
    in_specs = (P("tm", None, None, "slab"), P("slab"), P())
    out_specs = (P("tm", None, None), P("tm", None))
    return jax.shard_map(body, mesh=mesh, in_specs=in_specs, out_specs=out_specs, check_vma=False)
```

profile of v0, /device:TPU:0, one launch (start us, length us, event | category | flops | bytes accessed | tf_op | source)
XLA Modules:
  0.0 53.1 jit_solution(5413962570517012968)
XLA Ops:
  0.6 14.0 %all_gather.6 = bf16[4,3,2,16384]{3,2,1,0:T(2,128)(2,1)S(1)} all-gather(bf16[1,3,2,16384]{3,2,1,0:T(2,128)(2,1)} %param.7), channel_id=1, replica_groups=mesh['tm'=4,'slab'=8] {'tm'}, dimensions={0}, use_global_device_ids=true | all-gather | bytes 983040 | tf_op jit(solution)/shard_map/all_gather | solution.py:47
  14.6 6.1 %while.29 = (s32[]{:T(128)}, bf16[4,2,16384]{2,1,0:T(2,128)(2,1)S(1)}, bf16[3,2,16384]{2,1,0:T(2,128)(2,1)S(1)}, bf16[4,3,2,16384]{3,2,1,0:T(2,128)(2,1)S(1)}, s32[]{:T(128)}) while((s32[]{:T(128)}, bf16[4,2,16384]{2,1,0:T(2,128)(2,1)S(1)}, bf16[3,2,16384]{2,1,0:T(2,128)(2,1)S(1)}, bf16[4,3,2,16384]{3,2,1,0:T(2,128)(2,1)S(1)}, s32[]{:T(128)}) %tuple.65), condition=%wide.region_3.4_spmd, body=%wide.region_0.3_spmd.sunk | while | flops 884738 | bytes 2752585 | solution.py:55
  14.9 0.6 %fusion.31 = bf16[16384]{0:T(1024)(128)(2,1)S(1)} fusion(f32[3,2,16384]{2,1,0:T(2,128)S(1)} %bitcast_convert_fusion.2, f32[3,2,16384]{2,1,0:T(2,128)S(1)} %convert_element_type.58), kind=kLoop, calls=%fused_computation.6.clone.1 | loop fusion | flops 180224 | bytes 819200 | tf_op jit(solution)/shard_map/while/body/eval_jaxpr/reduce_sum | solution.py:38
  15.5 0.4 multiply_reduce_fusion.3
  15.9 0.2 maximum_dynamic-update-slice_fusion.2
  16.4 0.6 %fusion.31 = bf16[16384]{0:T(1024)(128)(2,1)S(1)} fusion(f32[3,2,16384]{2,1,0:T(2,128)S(1)} %bitcast_convert_fusion.2, f32[3,2,16384]{2,1,0:T(2,128)S(1)} %convert_element_type.58), kind=kLoop, calls=%fused_computation.6.clone.1 | loop fusion | flops 180224 | bytes 819200 | tf_op jit(solution)/shard_map/while/body/eval_jaxpr/reduce_sum | solution.py:38
  17.0 0.4 multiply_reduce_fusion.3
  17.5 0.2 maximum_dynamic-update-slice_fusion.2
  17.9 0.6 %fusion.31 = bf16[16384]{0:T(1024)(128)(2,1)S(1)} fusion(f32[3,2,16384]{2,1,0:T(2,128)S(1)} %bitcast_convert_fusion.2, f32[3,2,16384]{2,1,0:T(2,128)S(1)} %convert_element_type.58), kind=kLoop, calls=%fused_computation.6.clone.1 | loop fusion | flops 180224 | bytes 819200 | tf_op jit(solution)/shard_map/while/body/eval_jaxpr/reduce_sum | solution.py:38
  18.6 0.4 multiply_reduce_fusion.3
  19.0 0.2 maximum_dynamic-update-slice_fusion.2
  19.5 0.6 %fusion.31 = bf16[16384]{0:T(1024)(128)(2,1)S(1)} fusion(f32[3,2,16384]{2,1,0:T(2,128)S(1)} %bitcast_convert_fusion.2, f32[3,2,16384]{2,1,0:T(2,128)S(1)} %convert_element_type.58), kind=kLoop, calls=%fused_computation.6.clone.1 | loop fusion | flops 180224 | bytes 819200 | tf_op jit(solution)/shard_map/while/body/eval_jaxpr/reduce_sum | solution.py:38
  20.1 0.4 multiply_reduce_fusion.3
  20.5 0.2 maximum_dynamic-update-slice_fusion.2
  20.8 0.3 multiply_reduce_fusion.1
  21.2 8.8 %while.30 = (s32[]{:T(128)}, f32[8,128]{1,0:T(8,128)S(1)}, f32[1,128]{1,0:T(1,128)S(1)}, bf16[8,16384]{1,0:T(8,128)(2,1)S(1)}, s32[16384]{0:T(1024)}, /*index=5*...) while((s32[]{:T(128)}, f32[8,128]{1,0:T(8,128)S(1)}, ...), condition=%wide.region_6.7_spmd.clone, body=%wide.region_5.6_spmd.clone.sunk | while | flops 10488071 | bytes 156842 | solution.py:31
  21.2 0.7 %dynamic_slice.50 = s32[4096]{0:T(1024)S(1)} dynamic-slice(s32[16384]{0:T(1024)} %get-tuple-element.355, s32[]{:T(128)S(6)} %select_n.18), dynamic_slice_sizes={4096} | dynamic-slice | bytes 32772 | tf_op jit(solution)/shard_map/while/body/eval_jaxpr/dynamic_slice | solution.py:18
  21.9 0.7 %fusion.35 = f32[1,128]{1,0:T(1,128)S(1)} fusion(s32[4096]{0:T(1024)S(1)} %dynamic_slice.50, bf16[1,16384]{1,0:T(2,128)(2,1)S(1)} %get-tuple-element.356, s32[]{:T(128)S(6)} %select_n.18, f32[1,128]{1,0:T(1,128)S(1)} %get-tuple-element.343, pred[]{:T(512)S(6)} %compare.3), kind=kOutput, calls=%fused_computation.12.clone.1 | convolution fusion | flops 1573120 | bytes 33797 | tf_op jit(solution)/shard_map/while/body/eval_jaxpr/dot_general | solution.py:24
  22.7 0.7 %fusion.34 = f32[8,128]{1,0:T(8,128)S(1)} fusion(s32[4096]{0:T(1024)S(1)} %dynamic_slice.50, bf16[8,16384]{1,0:T(8,128)(2,1)S(1)} %get-tuple-element.354, s32[]{:T(128)S(6)} %select_n.18, f32[8,128]{1,0:T(8,128)S(1)} %get-tuple-element.342, pred[]{:T(512)S(6)} %compare.3), kind=kOutput, calls=%fused_computation.11.clone.1 | convolution fusion | flops 8914944 | bytes 90117 | tf_op jit(solution)/shard_map/while/body/eval_jaxpr/dot_general | solution.py:23
  23.4 0.7 %dynamic_slice.50 = s32[4096]{0:T(1024)S(1)} dynamic-slice(s32[16384]{0:T(1024)} %get-tuple-element.355, s32[]{:T(128)S(6)} %select_n.18), dynamic_slice_sizes={4096} | dynamic-slice | bytes 32772 | tf_op jit(solution)/shard_map/while/body/eval_jaxpr/dynamic_slice | solution.py:18
  24.1 0.7 %fusion.35 = f32[1,128]{1,0:T(1,128)S(1)} fusion(s32[4096]{0:T(1024)S(1)} %dynamic_slice.50, bf16[1,16384]{1,0:T(2,128)(2,1)S(1)} %get-tuple-element.356, s32[]{:T(128)S(6)} %select_n.18, f32[1,128]{1,0:T(1,128)S(1)} %get-tuple-element.343, pred[]{:T(512)S(6)} %compare.3), kind=kOutput, calls=%fused_computation.12.clone.1 | convolution fusion | flops 1573120 | bytes 33797 | tf_op jit(solution)/shard_map/while/body/eval_jaxpr/dot_general | solution.py:24
  24.8 0.7 %fusion.34 = f32[8,128]{1,0:T(8,128)S(1)} fusion(s32[4096]{0:T(1024)S(1)} %dynamic_slice.50, bf16[8,16384]{1,0:T(8,128)(2,1)S(1)} %get-tuple-element.354, s32[]{:T(128)S(6)} %select_n.18, f32[8,128]{1,0:T(8,128)S(1)} %get-tuple-element.342, pred[]{:T(512)S(6)} %compare.3), kind=kOutput, calls=%fused_computation.11.clone.1 | convolution fusion | flops 8914944 | bytes 90117 | tf_op jit(solution)/shard_map/while/body/eval_jaxpr/dot_general | solution.py:23
  25.6 0.7 %dynamic_slice.50 = s32[4096]{0:T(1024)S(1)} dynamic-slice(s32[16384]{0:T(1024)} %get-tuple-element.355, s32[]{:T(128)S(6)} %select_n.18), dynamic_slice_sizes={4096} | dynamic-slice | bytes 32772 | tf_op jit(solution)/shard_map/while/body/eval_jaxpr/dynamic_slice | solution.py:18
  26.3 0.7 %fusion.35 = f32[1,128]{1,0:T(1,128)S(1)} fusion(s32[4096]{0:T(1024)S(1)} %dynamic_slice.50, bf16[1,16384]{1,0:T(2,128)(2,1)S(1)} %get-tuple-element.356, s32[]{:T(128)S(6)} %select_n.18, f32[1,128]{1,0:T(1,128)S(1)} %get-tuple-element.343, pred[]{:T(512)S(6)} %compare.3), kind=kOutput, calls=%fused_computation.12.clone.1 | convolution fusion | flops 1573120 | bytes 33797 | tf_op jit(solution)/shard_map/while/body/eval_jaxpr/dot_general | solution.py:24
  27.0 0.7 %fusion.34 = f32[8,128]{1,0:T(8,128)S(1)} fusion(s32[4096]{0:T(1024)S(1)} %dynamic_slice.50, bf16[8,16384]{1,0:T(8,128)(2,1)S(1)} %get-tuple-element.354, s32[]{:T(128)S(6)} %select_n.18, f32[8,128]{1,0:T(8,128)S(1)} %get-tuple-element.342, pred[]{:T(512)S(6)} %compare.3), kind=kOutput, calls=%fused_computation.11.clone.1 | convolution fusion | flops 8914944 | bytes 90117 | tf_op jit(solution)/shard_map/while/body/eval_jaxpr/dot_general | solution.py:23
  27.8 0.7 %dynamic_slice.50 = s32[4096]{0:T(1024)S(1)} dynamic-slice(s32[16384]{0:T(1024)} %get-tuple-element.355, s32[]{:T(128)S(6)} %select_n.18), dynamic_slice_sizes={4096} | dynamic-slice | bytes 32772 | tf_op jit(solution)/shard_map/while/body/eval_jaxpr/dynamic_slice | solution.py:18
  28.5 0.7 %fusion.35 = f32[1,128]{1,0:T(1,128)S(1)} fusion(s32[4096]{0:T(1024)S(1)} %dynamic_slice.50, bf16[1,16384]{1,0:T(2,128)(2,1)S(1)} %get-tuple-element.356, s32[]{:T(128)S(6)} %select_n.18, f32[1,128]{1,0:T(1,128)S(1)} %get-tuple-element.343, pred[]{:T(512)S(6)} %compare.3), kind=kOutput, calls=%fused_computation.12.clone.1 | convolution fusion | flops 1573120 | bytes 33797 | tf_op jit(solution)/shard_map/while/body/eval_jaxpr/dot_general | solution.py:24
  29.2 0.7 %fusion.34 = f32[8,128]{1,0:T(8,128)S(1)} fusion(s32[4096]{0:T(1024)S(1)} %dynamic_slice.50, bf16[8,16384]{1,0:T(8,128)(2,1)S(1)} %get-tuple-element.354, s32[]{:T(128)S(6)} %select_n.18, f32[8,128]{1,0:T(8,128)S(1)} %get-tuple-element.342, pred[]{:T(512)S(6)} %compare.3), kind=kOutput, calls=%fused_computation.11.clone.1 | convolution fusion | flops 8914944 | bytes 90117 | tf_op jit(solution)/shard_map/while/body/eval_jaxpr/dot_general | solution.py:23
  29.9 15.7 %all-reduce = (f32[1,128]{1,0:T(1,128)S(1)}, f32[4,2,128]{2,0,1:T(4,128)S(1)}) all-reduce(f32[1,128]{1,0:T(1,128)S(1)} %get-tuple-element.208, f32[4,2,128]{2,0,1:T(4,128)S(1)} %copy.6), channel_id=1, replica_groups=mesh['tm'=4,'slab'=8] {'slab'}, use_global_device_ids=true, to_apply=%region_8.9 | all-reduce | flops 1152 | bytes 9216 | tf_op jit(solution)/shard_map/psum | solution.py:61
  45.7 6.4 %all-gather = f32[4,1,128]{2,1,0:T(1,128)S(1)} all-gather(f32[1,1,128]{2,1,0:T(1,128)S(1)} %bitcast.36), channel_id=1, replica_groups=mesh['tm'=4,'slab'=8] {'tm'}, dimensions={0}, use_global_device_ids=true | all-gather | bytes 2560 | tf_op jit(solution)/shard_map/all_gather | solution.py:62
  52.1 0.2 fusion.20
  52.3 0.8 %fusion.16 = f32[1,4,128]{2,1,0:T(4,128)} fusion(f32[4,128]{1,0:T(4,128)S(1)} %bitcast.35, f32[4,2,128]{2,0,1:T(4,128)S(1)} %fusion.20, f32[128]{0:T(128)S(1)} %bitcast.37, s32[4]{0:T(128)S(1)} %copy-done.2), kind=kOutput, calls=%fused_computation.23 | convolution fusion | flops 27152 | bytes 8720 | tf_op jit(solution)/shard_map/dot_general | solution.py:72
  (28 shorter events, 1.6 us)
Async XLA Ops:
  0.6 14.0 %copy-start = (bf16[1,3,2,16384]{3,2,1,0:T(2,128)(2,1)S(1)}, bf16[1,3,2,16384]{3,2,1,0:T(2,128)(2,1)}, u32[]{:S(2)}) copy-start(bf16[1,3,2,16384]{3,2,1,0:T(2,128)(2,1)} %param.7) | copy-start | bytes 589828
  21.2 30.9 %copy-start.2 = (s32[4]{0:T(128)S(1)}, s32[4]{0:T(128)}, u32[]{:S(2)}) copy-start(s32[4]{0:T(128)} %param.9) | copy-start | bytes 52
  45.7 7.4 %copy-start.1 = (f32[1,128]{1,0:T(1,128)}, f32[1,128]{1,0:T(1,128)S(1)}, u32[]{:S(2)}) copy-start(f32[1,128]{1,0:T(1,128)S(1)} %get-tuple-element.252) | copy-start | bytes 1540
where the time goes:
time: 53.6 us; the launch traced here: 53.1 us
  blocking collectives  36.1 us (67%)
  matrix products  6.79 us (13%)
  other arithmetic  5.92 us (11%)
  local copies, waits for them, and re-layouts  3.37 us (6%)
  between operations  0.7 us (1%)
    psum x1, blocking collectives, body(): lax.psum((partial_cross, partial_energy), 'slab')  15.7 us
    all_gather x1, blocking collectives, body(): pieces = lax.all_gather(velocity, 'tm', axis=0, tiled=True)  14 us
    all_gather x1, blocking collectives, body(): all_spectra = lax.all_gather(own_spectrum, 'tm', axis=0, tiled=True)  6.42 us
    dot_general x4, matrix products, add_block(): jnp.dot(cross_block, onehot, preferred_element_type=jnp.float32)  2.91 us
    dynamic_slice x4, local copies, waits for them, and re-layouts, add_block(): block_ids = lax.dynamic_slice_in_dim(shell_ids, first_row, block_size, 0)  2.91 us
    dot_general x4, matrix products, add_block(): jnp.dot(energy_block, onehot, preferred_element_type=jnp.float32)  2.91 us
    reduce_sum x4, other arithmetic, pair_terms(): jnp.sum(own_wide[:, 1] * ref_wide[:, 0] - own_wide[:, 0] * ref_wide[:, 1]...  2.29 us
    reduce_sum x4, other arithmetic, pair_terms(): real_part = jnp.sum(own_wide * ref_wide, axis=(0, 1))  1.51 us

commit v1 on v0

v1 whole, which is shorter than its diff:
```python
import functools

import jax
import jax.numpy as jnp
from jax import lax
from jax.experimental import pallas as pl
from jax.experimental.pallas import tpu as pltpu
from jax.sharding import PartitionSpec as P

SHELLS = 128
LANES = 128
CORES = 2
MESH = pl.DeviceIdType.MESH


def kernel(
    snaps, slabs, rows,
    vel_ref, ids_ref, order_ref,
    coh_ref, spec_ref,
    staged, ids, got, split, terms, lhs, hot, mine, near, mid, far, total, ready,
    load_sem, send_sem, recv_sem, near_send, near_recv, far_send, far_recv,
):
    tm = lax.axis_index("tm")
    slab = lax.axis_index("slab")
    core = lax.rem(slab, CORES)
    place = lax.div(slab, CORES)
    places = slabs // CORES
    pairs = snaps * snaps

    load_vel = pltpu.make_async_copy(vel_ref, staged, load_sem.at[0])
    load_vel.start()
    load_ids = pltpu.make_async_copy(
        ids_ref.at[pl.ds(pl.multiple_of(tm * rows, rows), rows)], ids, load_sem.at[1]
    )
    load_ids.start()
    own = pl.ds(pl.multiple_of(tm * 2 * rows, 2 * rows), 2 * rows)
    load_own = pltpu.make_async_copy(vel_ref.at[:, own], got.at[tm], load_sem.at[2])
    load_own.start()

    near_peers = []
    for offset in range(1, snaps * CORES):
        other = lax.rem(tm + offset // CORES, snaps)
        other_core = lax.rem(core + offset % CORES, CORES)
        near_peers.append((other, place * CORES + other_core))
    far_peers = []
    for offset in range(1, places):
        far_peers.append((tm, lax.rem(place + offset, places) * CORES + core))

    barrier = pltpu.get_barrier_semaphore()
    for peer in near_peers + far_peers:
        pl.semaphore_signal(barrier, inc=1, device_id=peer, device_id_type=MESH)

    load_ids.wait()
    shell = lax.broadcasted_iota(jnp.int32, (SHELLS, LANES), 0)
    for j in range(rows):
        same = shell == jnp.broadcast_to(ids[j : j + 1, :], (SHELLS, LANES))
        hot[:, j * LANES : (j + 1) * LANES] = jnp.where(same, 1.0, 0.0).astype(jnp.bfloat16)

    load_vel.wait()
    pl.semaphore_wait(barrier, len(near_peers) + len(far_peers))

    moves = []
    for offset in range(1, snaps):
        other = lax.rem(tm + offset, snaps)
        share = pl.ds(pl.multiple_of(other * 2 * rows, 2 * rows), 2 * rows)
        move = pltpu.make_async_remote_copy(
            src_ref=staged.at[:, share],
            dst_ref=got.at[tm],
            send_sem=send_sem.at[offset],
            recv_sem=recv_sem.at[offset],
            device_id=(other, slab),
            device_id_type=MESH,
        )
        move.start()
        moves.append(move)
    load_own.wait()
    for move in moves:
        move.wait()

    real, imag = {}, {}
    for t in range(snaps):
        for c in range(3):
            split[t * 3 + c] = got[t, c].astype(jnp.float32)
    for t in range(snaps):
        for c in range(3):
            real[t, c] = split[t * 3 + c, pl.ds(0, rows, stride=2), :]
            imag[t, c] = split[t * 3 + c, pl.ds(1, rows, stride=2), :]

    for t in range(snaps):
        for r in range(t, snaps):
            value = real[t, 0] * real[r, 0] + imag[t, 0] * imag[r, 0]
            for c in (1, 2):
                value = value + real[t, c] * real[r, c]
                value = value + imag[t, c] * imag[r, c]
            terms[(t * snaps + r) * rows : (t * snaps + r + 1) * rows] = value
            if r > t:
                value = imag[t, 0] * real[r, 0] - real[t, 0] * imag[r, 0]
                for c in (1, 2):
                    value = value + imag[t, c] * real[r, c]
                    value = value - real[t, c] * imag[r, c]
                terms[(r * snaps + t) * rows : (r * snaps + t + 1) * rows] = value
    for j in range(rows):
        block = terms[pl.ds(j, pairs, stride=rows), :]
        lhs[:, j * LANES : (j + 1) * LANES] = block.astype(jnp.bfloat16)
    mine[...] = lax.dot_general(
        lhs[...], hot[...], (((1,), (1,)), ((), ())), preferred_element_type=jnp.float32
    )

    def spread(source, slots, slot_of_me, peers, send, recv):
        copies = []
        for n, peer in enumerate(peers):
            copy = pltpu.make_async_remote_copy(
                src_ref=source,
                dst_ref=slots.at[n],
                send_sem=send.at[n],
                recv_sem=recv.at[n],
                device_id=peer,
                device_id_type=MESH,
            )
            copy.start()
            copies.append(copy)
        for copy in copies:
            copy.wait()
        value = source[...]
        for n in range(len(peers)):
            value = value + slots[n]
        return value

    mid[...] = spread(mine, near, None, near_peers, near_send, near_recv)
    total[...] = spread(mid, far, None, far_peers, far_send, far_recv)

    spectra = total[pl.ds(0, snaps, stride=snaps + 1), :]
    own_spectrum = total[pl.ds(tm * (snaps + 1), 1), :]
    across = total[pl.ds(tm * snaps, snaps), :]
    down = total[pl.ds(tm, snaps, stride=snaps), :]
    which = lax.broadcasted_iota(jnp.int32, (snaps, SHELLS), 0)
    down = jnp.where(which == tm, 0.0, down)
    ready[...] = (across * across + down * down) / (own_spectrum * spectra)
    for j in range(snaps):
        coh_ref[0, j : j + 1, :] = ready[pl.ds(order_ref[j], 1), :]
    spec_ref[...] = own_spectrum


def body(velocity, shell_index, ref_order):
    snaps = lax.axis_size("tm")
    slabs = lax.axis_size("slab")
    modes = velocity.shape[3]
    blocks = modes // LANES
    rows = blocks // snaps
    pairs = snaps * snaps
    vel = velocity.reshape(3, 2, blocks, LANES).transpose(0, 2, 1, 3)
    vel = vel.reshape(3, 2 * blocks, LANES)
    ids = shell_index.reshape(blocks, LANES)
    near = snaps * CORES - 1
    far = slabs // CORES - 1
    return pl.pallas_call(
        functools.partial(kernel, snaps, slabs, rows),
        out_shape=(
            jax.ShapeDtypeStruct((1, snaps, SHELLS), jnp.float32),
            jax.ShapeDtypeStruct((1, SHELLS), jnp.float32),
        ),
        in_specs=[
            pl.BlockSpec(memory_space=pl.ANY),
            pl.BlockSpec(memory_space=pl.ANY),
            pl.BlockSpec(memory_space=pltpu.SMEM),
        ],
        out_specs=(
            pl.BlockSpec(memory_space=pltpu.VMEM),
            pl.BlockSpec(memory_space=pltpu.VMEM),
        ),
        scratch_shapes=[
            pltpu.VMEM((3, 2 * blocks, LANES), jnp.bfloat16),
            pltpu.VMEM((rows, LANES), jnp.int32),
            pltpu.VMEM((snaps, 3, 2 * rows, LANES), jnp.bfloat16),
            pltpu.VMEM((snaps * 3, 2 * rows, LANES), jnp.float32),
            pltpu.VMEM((pairs * rows, LANES), jnp.float32),
            pltpu.VMEM((pairs, rows * LANES), jnp.bfloat16),
            pltpu.VMEM((SHELLS, rows * LANES), jnp.bfloat16),
            pltpu.VMEM((pairs, SHELLS), jnp.float32),
            pltpu.VMEM((near, pairs, SHELLS), jnp.float32),
            pltpu.VMEM((pairs, SHELLS), jnp.float32),
            pltpu.VMEM((far, pairs, SHELLS), jnp.float32),
            pltpu.VMEM((pairs, SHELLS), jnp.float32),
            pltpu.VMEM((snaps, SHELLS), jnp.float32),
            pltpu.SemaphoreType.DMA((3,)),
            pltpu.SemaphoreType.DMA((snaps,)),
            pltpu.SemaphoreType.DMA((snaps,)),
            pltpu.SemaphoreType.DMA((near,)),
            pltpu.SemaphoreType.DMA((near,)),
            pltpu.SemaphoreType.DMA((far,)),
            pltpu.SemaphoreType.DMA((far,)),
        ],
        compiler_params=pltpu.CompilerParams(collective_id=0, has_side_effects=True),
    )(vel, ids, ref_order)


def solution(mesh):
    in_specs = (P("tm", None, None, "slab"), P("slab"), P())
    out_specs = (P("tm", None, None), P("tm", None))
    return jax.shard_map(body, mesh=mesh, in_specs=in_specs, out_specs=out_specs, check_vma=False)
```

time: 53.6 us -> 21.6 us (0.40)
  blocking collectives: 36.1 us -> 0 us
  Pallas kernels: 0 us -> 18.9 us
  matrix products: 6.79 us -> 0 us
  other arithmetic: 5.92 us -> 0 us
  local copies, waits for them, and re-layouts: 3.37 us -> 1.8 us
    all_gather x2 -> x0, blocking collectives: 20.4 us -> none  [the longest x1 14 us: body(): pieces = lax.all_gather(velocity, 'tm', axis=0, tiled=True)]
    pallas_call x0 -> x1, Pallas kernels: none -> 18.9 us  [body(): pl.pallas_call(functools.partial(kernel, snaps, slabs, rows), out_shape=(...]
    psum x1 -> x0, blocking collectives: 15.7 us -> none  [body(): lax.psum((partial_cross, partial_energy), 'slab')]
    dot_general x10 -> x0, matrix products: 6.79 us -> none  [the longest x4 2.91 us: add_block(): jnp.dot(cross_block, onehot, preferred_element_type=jnp.float32)]
    reduce_sum x9 -> x0, other arithmetic: 4.11 us -> none  [the longest x4 2.29 us: pair_terms(): jnp.sum(own_wide[:, 1] * ref_wide[:, 0] - own_wide[:, 0] * ref_wide[:, 1]...]
    dynamic_slice x4 -> x0, local copies, waits for them, and re-layouts: 2.91 us -> none  [add_block(): block_ids = lax.dynamic_slice_in_dim(shell_ids, first_row, block_size, 0)]
    unnamed x6, local copies, waits for them, and re-layouts: 0.02 us -> 1.8 us
    convert_element_type x8 -> x0, other arithmetic: 1.12 us -> none  [the longest x4 0.57 us: pair_terms(): ref_wide = ref_modes.astype(jnp.float32)]
where the time goes in v1:
time: 21.6 us; the launch traced here: 21.4 us
  Pallas kernels  18.9 us (87%)
  local copies, waits for them, and re-layouts  1.8 us (8%)
  between operations  0.65 us (3%)
    pallas_call x1, Pallas kernels, body(): pl.pallas_call(functools.partial(kernel, snaps, slabs, rows), out_shape=(...  18.9 us
    unnamed x6, local copies, waits for them, and re-layouts  1.8 us

profile of v1, /device:TPU:0, one launch (start us, length us, event | category | flops | bytes accessed | tf_op | source)
XLA Modules:
  0.0 21.4 jit_solution(2813761643998561679)
XLA Ops:
  0.6 18.9 %shard_map.50 = (f32[1,4,128]{2,1,0:T(4,128)}, f32[1,128]{1,0:T(1,128)}) custom-call(bf16[3,256,128]{2,1,0:T(8,128)(2,1)} %bitcast.6, s32[128,128]{1,0:T(8,128)} %bitcast.7, s32[4]{0:T(128)} %order_ref.1), custom_call_target="tpu_custom_call" | custom-call | tf_op jit(solution)/shard_map/pallas_call | solution.py:156
  19.6 0.0 copy-start
  19.6 0.7 %copy-done = f32[1,4,128]{2,1,0:T(4,128)S(1)} copy-done((f32[1,4,128]{2,1,0:T(4,128)S(1)}, f32[1,4,128]{2,1,0:T(4,128)}, u32[]{:S(2)}) %copy-start) | copy-done | bytes 2072
  20.2 0.0 copy-start.1
  20.2 0.6 %copy.8 = f32[1,4,128]{2,1,0:T(4,128)} copy(f32[1,4,128]{2,1,0:T(4,128)S(1)} %copy-done) | data formatting | bytes 4096
  20.8 0.1 copy-done.1
  20.9 0.5 %copy.9 = f32[1,128]{1,0:T(1,128)} copy(f32[1,128]{1,0:T(1,128)S(1)} %copy-done.1) | data formatting | bytes 1024
Async XLA Ops:
  19.6 0.7 %copy-start = (f32[1,4,128]{2,1,0:T(4,128)S(1)}, f32[1,4,128]{2,1,0:T(4,128)}, u32[]{:S(2)}) copy-start(f32[1,4,128]{2,1,0:T(4,128)} %get-tuple-element.4) | copy-start | bytes 6148
  20.2 0.6 %copy-start.1 = (f32[1,128]{1,0:T(1,128)S(1)}, f32[1,128]{1,0:T(1,128)}, u32[]{:S(2)}) copy-start(f32[1,128]{1,0:T(1,128)} %get-tuple-element.5) | copy-start | bytes 1540

commit v2 on v1

v2 whole, which is shorter than its diff:
```python
import functools

import jax
import jax.numpy as jnp
from jax import lax
from jax.experimental import pallas as pl
from jax.experimental.pallas import tpu as pltpu
from jax.sharding import PartitionSpec as P

SHELLS = 128
LANES = 128
CORES = 2
MESH = pl.DeviceIdType.MESH


def kernel(
    snaps, slabs, rows,
    vel_ref, ids_ref, order_ref,
    coh_ref, spec_ref,
    staged, ids, order, got, split, terms, lhs, hot, mine, packs, near, mid, far, total, ready,
    load_sem, stage_sem, send_sem, recv_sem, near_send, near_recv, far_send, far_recv,
):
    tm = lax.axis_index("tm")
    slab = lax.axis_index("slab")
    core = lax.rem(slab, CORES)
    place = lax.div(slab, CORES)
    places = slabs // CORES
    pairs = snaps * snaps
    half = 3 * snaps // CORES

    others = []
    for high in reversed(range(snaps // 2)):
        for low in (1, 0):
            other_high = lax.rem(lax.div(tm, 2) + high, snaps // 2)
            others.append(other_high * 2 + lax.rem(lax.rem(tm, 2) + low, 2))
    others = others[:-1]
    other_core = CORES - 1 - core
    near_peers = [(other, other_core, 1) for other in others]
    near_peers += [(other, core, 0) for other in others]
    near_peers += [(tm, other_core, 1)]
    far_peers = []
    for offset in range(1, places):
        away = lax.rem(place + offset, places)
        far_peers += [(away, other_core, 1), (away, core, 0)]
    far_peers += [(place, other_core, 1)]

    barrier = pltpu.get_barrier_semaphore()
    for away, to_core, _ in far_peers[:-1]:
        pl.semaphore_signal(
            barrier, inc=1, device_id=(tm, away * CORES + to_core), device_id_type=MESH
        )
    for other, to_core, _ in near_peers:
        pl.semaphore_signal(
            barrier, inc=1, device_id=(other, place * CORES + to_core), device_id_type=MESH
        )

    def share_of(snap):
        return pl.ds(pl.multiple_of(snap * 2 * rows, 2 * rows), 2 * rows)

    stages = []
    for n, other in enumerate(others):
        stage = pltpu.make_async_copy(
            vel_ref.at[:, share_of(other)], staged.at[n], stage_sem.at[n]
        )
        stage.start()
        stages.append(stage)
    load_own = pltpu.make_async_copy(vel_ref.at[:, share_of(tm)], got.at[tm], load_sem.at[0])
    load_own.start()
    load_ids = pltpu.make_async_copy(
        ids_ref.at[pl.ds(pl.multiple_of(tm * rows, rows), rows)], ids, load_sem.at[1]
    )
    load_ids.start()
    load_order = pltpu.make_async_copy(order_ref, order, load_sem.at[2])
    load_order.start()

    pl.semaphore_wait(barrier, len(near_peers) + len(far_peers) - 1)
    moves = []
    for n, other in enumerate(others):
        stages[n].wait()
        move = pltpu.make_async_remote_copy(
            src_ref=staged.at[n],
            dst_ref=got.at[tm],
            send_sem=send_sem.at[n],
            recv_sem=recv_sem.at[n],
            device_id=(other, slab),
            device_id_type=MESH,
        )
        move.start()
        moves.append(move)

    load_ids.wait()
    shell = lax.broadcasted_iota(jnp.int32, (SHELLS, LANES), 0)
    for j in range(rows):
        same = shell == jnp.broadcast_to(ids[j : j + 1, :], (SHELLS, LANES))
        hot[:, j * LANES : (j + 1) * LANES] = jnp.where(same, 1.0, 0.0).astype(jnp.bfloat16)

    load_order.wait()
    load_own.wait()
    for move in moves:
        move.wait()

    real, imag = {}, {}
    for t in range(snaps):
        for c in range(3):
            split[t * 3 + c] = got[t, c].astype(jnp.float32)
    for t in range(snaps):
        for c in range(3):
            real[t, c] = split[t * 3 + c, pl.ds(0, rows, stride=2), :]
            imag[t, c] = split[t * 3 + c, pl.ds(1, rows, stride=2), :]

    for t in range(snaps):
        for r in range(t, snaps):
            value = real[t, 0] * real[r, 0] + imag[t, 0] * imag[r, 0]
            for c in (1, 2):
                value = value + real[t, c] * real[r, c]
                value = value + imag[t, c] * imag[r, c]
            terms[(t * snaps + r) * rows : (t * snaps + r + 1) * rows] = value
            if r > t:
                value = imag[t, 0] * real[r, 0] - real[t, 0] * imag[r, 0]
                for c in (1, 2):
                    value = value + imag[t, c] * real[r, c]
                    value = value - real[t, c] * imag[r, c]
                terms[(r * snaps + t) * rows : (r * snaps + t + 1) * rows] = value
    for j in range(rows):
        block = terms[pl.ds(j, pairs, stride=rows), :]
        lhs[:, j * LANES : (j + 1) * LANES] = block.astype(jnp.bfloat16)
    mine[...] = lax.dot_general(
        lhs[...], hot[...], (((1,), (1,)), ((), ())), preferred_element_type=jnp.float32
    )

    mid_rows = snaps // 2
    for t in range(snaps):
        packs[t, 0, :snaps] = mine[t * snaps : (t + 1) * snaps, :]
        packs[t, 0, snaps:half] = mine[pl.ds(t, mid_rows, stride=snaps), :]
        packs[t, 1, :mid_rows] = mine[pl.ds(t + mid_rows * snaps, mid_rows, stride=snaps), :]
        packs[t, 1, mid_rows:half] = mine[pl.ds(0, snaps, stride=snaps + 1), :]

    copies = []
    for n, (other, to_core, _) in enumerate(near_peers):
        copy = pltpu.make_async_remote_copy(
            src_ref=packs.at[other, to_core],
            dst_ref=near.at[n],
            send_sem=near_send.at[n],
            recv_sem=near_recv.at[n],
            device_id=(other, place * CORES + to_core),
            device_id_type=MESH,
        )
        copy.start()
        copies.append(copy)
    value = packs[tm, core]
    for n in reversed(range(len(near_peers))):
        copies[n].wait()
        value = value + near[n]
    mid[...] = value

    copies = []
    for n, (away, to_core, _) in enumerate(far_peers):
        copy = pltpu.make_async_remote_copy(
            src_ref=mid,
            dst_ref=far.at[n],
            send_sem=far_send.at[n],
            recv_sem=far_recv.at[n],
            device_id=(tm, away * CORES + to_core),
            device_id_type=MESH,
        )
        copy.start()
        copies.append(copy)
    sums = [mid[...], None]
    for n in reversed(range(len(far_peers))):
        copies[n].wait()
        turn = far_peers[n][2]
        sums[turn] = far[n] if sums[turn] is None else sums[turn] + far[n]
    total[core] = sums[0]
    total[other_core] = sums[1]

    across = total[0, :snaps]
    own_spectrum = total[0, pl.ds(tm, 1), :]
    ready[:mid_rows] = total[0, snaps:half]
    ready[mid_rows:] = total[1, :mid_rows]
    down = ready[...]
    spectra = total[1, mid_rows:half]
    which = lax.broadcasted_iota(jnp.int32, (snaps, SHELLS), 0)
    down = jnp.where(which == tm, 0.0, down)
    ready[...] = (across * across + down * down) / (own_spectrum * spectra)
    for j in range(snaps):
        coh_ref[0, j : j + 1, :] = ready[pl.ds(order[j], 1), :]
    spec_ref[...] = own_spectrum


def body(velocity, shell_index, ref_order):
    snaps = lax.axis_size("tm")
    slabs = lax.axis_size("slab")
    modes = velocity.shape[3]
    blocks = modes // LANES
    rows = blocks // snaps
    pairs = snaps * snaps
    vel = velocity.reshape(3, 2, blocks, LANES).transpose(0, 2, 1, 3)
    vel = vel.reshape(3, 2 * blocks, LANES)
    ids = shell_index.reshape(blocks, LANES)
    near = snaps * CORES - 1
    far = slabs - 1
    half = 3 * snaps // CORES
    return pl.pallas_call(
        functools.partial(kernel, snaps, slabs, rows),
        out_shape=(
            pltpu.VMEM((1, snaps, SHELLS), jnp.float32),
            pltpu.VMEM((1, SHELLS), jnp.float32),
        ),
        in_specs=[
            pl.BlockSpec(memory_space=pl.ANY),
            pl.BlockSpec(memory_space=pl.ANY),
            pl.BlockSpec(memory_space=pl.ANY),
        ],
        out_specs=(
            pl.BlockSpec(memory_space=pltpu.VMEM),
            pl.BlockSpec(memory_space=pltpu.VMEM),
        ),
        scratch_shapes=[
            pltpu.VMEM((snaps - 1, 3, 2 * rows, LANES), jnp.bfloat16),
            pltpu.VMEM((rows, LANES), jnp.int32),
            pltpu.SMEM((snaps,), jnp.int32),
            pltpu.VMEM((snaps, 3, 2 * rows, LANES), jnp.bfloat16),
            pltpu.VMEM((snaps * 3, 2 * rows, LANES), jnp.float32),
            pltpu.VMEM((pairs * rows, LANES), jnp.float32),
            pltpu.VMEM((pairs, rows * LANES), jnp.bfloat16),
            pltpu.VMEM((SHELLS, rows * LANES), jnp.bfloat16),
            pltpu.VMEM((pairs, SHELLS), jnp.float32),
            pltpu.VMEM((snaps, CORES, half, SHELLS), jnp.float32),
            pltpu.VMEM((near, half, SHELLS), jnp.float32),
            pltpu.VMEM((half, SHELLS), jnp.float32),
            pltpu.VMEM((far, half, SHELLS), jnp.float32),
            pltpu.VMEM((CORES, half, SHELLS), jnp.float32),
            pltpu.VMEM((snaps, SHELLS), jnp.float32),
            pltpu.SemaphoreType.DMA((3,)),
            pltpu.SemaphoreType.DMA((snaps - 1,)),
            pltpu.SemaphoreType.DMA((snaps - 1,)),
            pltpu.SemaphoreType.DMA((snaps - 1,)),
            pltpu.SemaphoreType.DMA((near,)),
            pltpu.SemaphoreType.DMA((near,)),
            pltpu.SemaphoreType.DMA((far,)),
            pltpu.SemaphoreType.DMA((far,)),
        ],
        compiler_params=pltpu.CompilerParams(collective_id=0, has_side_effects=True),
    )(vel, ids, ref_order)


def solution(mesh):
    in_specs = (P("tm", None, None, "slab"), P("slab"), P())
    out_specs = (P("tm", None, None), P("tm", None))
    return jax.shard_map(body, mesh=mesh, in_specs=in_specs, out_specs=out_specs, check_vma=False)
```

time: 21.6 us -> 19.1 us (0.88)
  Pallas kernels: 18.9 us -> 17.3 us
  local copies, waits for them, and re-layouts: 1.8 us -> 1.09 us
    pallas_call x1, Pallas kernels: 18.9 us -> 17.3 us  [body(): pl.pallas_call(functools.partial(kernel, snaps, slabs, rows), out_shape=(...]
    unnamed x6 -> x2, local copies, waits for them, and re-layouts: 1.8 us -> 1.09 us
where the time goes in v2:
time: 19.1 us; the launch traced here: 19 us
  Pallas kernels  17.3 us (91%)
  local copies, waits for them, and re-layouts  1.09 us (6%)
  between operations  0.64 us (3%)
    pallas_call x1, Pallas kernels, body(): pl.pallas_call(functools.partial(kernel, snaps, slabs, rows), out_shape=(...  17.3 us
    unnamed x2, local copies, waits for them, and re-layouts  1.09 us

profile of v2, /device:TPU:0, one launch (start us, length us, event | category | flops | bytes accessed | tf_op | source)
XLA Modules:
  0.0 19.0 jit_solution(13447501024358540644)
XLA Ops:
  0.6 17.3 %shard_map.50 = (f32[1,4,128]{2,1,0:T(4,128)S(1)}, f32[1,128]{1,0:T(1,128)S(1)}) custom-call(bf16[3,256,128]{2,1,0:T(8,128)(2,1)} %bitcast.6, s32[128,128]{1,0:T(8,128)} %bitcast.7, s32[4]{0:T(128)} %order_ref.1), custom_call_target="tpu_custom_call" | custom-call | tf_op jit(solution)/shard_map/pallas_call | solution.py:203
  17.9 0.6 %copy.8 = f32[1,4,128]{2,1,0:T(4,128)} copy(f32[1,4,128]{2,1,0:T(4,128)S(1)} %get-tuple-element.2) | data formatting | bytes 4096
  18.5 0.5 %copy.9 = f32[1,128]{1,0:T(1,128)} copy(f32[1,128]{1,0:T(1,128)S(1)} %get-tuple-element.3) | data formatting | bytes 1024

commit v3 on v2

--- a/solution.py
+++ b/solution.py
@@ -57,13 +57,8 @@
     def share_of(snap):
         return pl.ds(pl.multiple_of(snap * 2 * rows, 2 * rows), 2 * rows)
 
-    stages = []
     for n, other in enumerate(others):
-        stage = pltpu.make_async_copy(
-            vel_ref.at[:, share_of(other)], staged.at[n], stage_sem.at[n]
-        )
-        stage.start()
-        stages.append(stage)
+        pltpu.make_async_copy(vel_ref.at[:, share_of(other)], staged.at[n], stage_sem).start()
     load_own = pltpu.make_async_copy(vel_ref.at[:, share_of(tm)], got.at[tm], load_sem.at[0])
     load_own.start()
     load_ids = pltpu.make_async_copy(
@@ -74,19 +69,17 @@
     load_order.start()
 
     pl.semaphore_wait(barrier, len(near_peers) + len(far_peers) - 1)
-    moves = []
+    pltpu.make_async_copy(staged, staged, stage_sem).wait()
     for n, other in enumerate(others):
-        stages[n].wait()
         move = pltpu.make_async_remote_copy(
             src_ref=staged.at[n],
             dst_ref=got.at[tm],
-            send_sem=send_sem.at[n],
-            recv_sem=recv_sem.at[n],
+            send_sem=send_sem,
+            recv_sem=recv_sem,
             device_id=(other, slab),
             device_id_type=MESH,
         )
         move.start()
-        moves.append(move)
 
     load_ids.wait()
     shell = lax.broadcasted_iota(jnp.int32, (SHELLS, LANES), 0)
@@ -96,8 +89,7 @@
 
     load_order.wait()
     load_own.wait()
-    for move in moves:
-        move.wait()
+    pltpu.make_async_copy(staged, staged, recv_sem).wait()
 
     real, imag = {}, {}
     for t in range(snaps):
@@ -135,41 +127,38 @@
         packs[t, 1, :mid_rows] = mine[pl.ds(t + mid_rows * snaps, mid_rows, stride=snaps), :]
         packs[t, 1, mid_rows:half] = mine[pl.ds(0, snaps, stride=snaps + 1), :]
 
-    copies = []
     for n, (other, to_core, _) in enumerate(near_peers):
         copy = pltpu.make_async_remote_copy(
             src_ref=packs.at[other, to_core],
-            dst_ref=near.at[n],
-            send_sem=near_send.at[n],
-            recv_sem=near_recv.at[n],
+            dst_ref=near.at[n * half : (n + 1) * half],
+            send_sem=near_send,
+            recv_sem=near_recv,
             device_id=(other, place * CORES + to_core),
             device_id_type=MESH,
         )
         copy.start()
-        copies.append(copy)
     value = packs[tm, core]
-    for n in reversed(range(len(near_peers))):
-        copies[n].wait()
-        value = value + near[n]
+    pltpu.make_async_copy(near, near, near_recv).wait()
+    for n in range(len(near_peers)):
+        value = value + near[n * half : (n + 1) * half]
     mid[...] = value
 
-    copies = []
     for n, (away, to_core, _) in enumerate(far_peers):
         copy = pltpu.make_async_remote_copy(
             src_ref=mid,
-            dst_ref=far.at[n],
-            send_sem=far_send.at[n],
-            recv_sem=far_recv.at[n],
+            dst_ref=far.at[n * half : (n + 1) * half],
+            send_sem=far_send,
+            recv_sem=far_recv,
             device_id=(tm, away * CORES + to_core),
             device_id_type=MESH,
         )
         copy.start()
-        copies.append(copy)
     sums = [mid[...], None]
-    for n in reversed(range(len(far_peers))):
-        copies[n].wait()
+    pltpu.make_async_copy(far, far, far_recv).wait()
+    for n in range(len(far_peers)):
         turn = far_peers[n][2]
-        sums[turn] = far[n] if sums[turn] is None else sums[turn] + far[n]
+        term = far[n * half : (n + 1) * half]
+        sums[turn] = term if sums[turn] is None else sums[turn] + term
     total[core] = sums[0]
     total[other_core] = sums[1]
 
@@ -185,6 +174,20 @@
     for j in range(snaps):
         coh_ref[0, j : j + 1, :] = ready[pl.ds(order[j], 1), :]
     spec_ref[...] = own_spectrum
+    pltpu.make_async_copy(staged, staged, send_sem).wait()
+    pltpu.make_async_copy(near, near, near_send).wait()
+    pltpu.make_async_copy(far, far, far_send).wait()
+
+
+def put(coh_ref, spec_ref, coh_out, spec_out, sems):
+    copies = [
+        pltpu.make_async_copy(coh_ref, coh_out, sems.at[0]),
+        pltpu.make_async_copy(spec_ref, spec_out, sems.at[1]),
+    ]
+    for copy in copies:
+        copy.start()
+    for copy in copies:
+        copy.wait()
 
 
 def body(velocity, shell_index, ref_order):
@@ -200,7 +203,7 @@
     near = snaps * CORES - 1
     far = slabs - 1
     half = 3 * snaps // CORES
-    return pl.pallas_call(
+    coherence, spectrum = pl.pallas_call(
         functools.partial(kernel, snaps, slabs, rows),
         out_shape=(
             pltpu.VMEM((1, snaps, SHELLS), jnp.float32),
@@ -226,22 +229,34 @@
             pltpu.VMEM((SHELLS, rows * LANES), jnp.bfloat16),
             pltpu.VMEM((pairs, SHELLS), jnp.float32),
             pltpu.VMEM((snaps, CORES, half, SHELLS), jnp.float32),
-            pltpu.VMEM((near, half, SHELLS), jnp.float32),
+            pltpu.VMEM((near * half, SHELLS), jnp.float32),
             pltpu.VMEM((half, SHELLS), jnp.float32),
-            pltpu.VMEM((far, half, SHELLS), jnp.float32),
+            pltpu.VMEM((far * half, SHELLS), jnp.float32),
             pltpu.VMEM((CORES, half, SHELLS), jnp.float32),
             pltpu.VMEM((snaps, SHELLS), jnp.float32),
             pltpu.SemaphoreType.DMA((3,)),
-            pltpu.SemaphoreType.DMA((snaps - 1,)),
-            pltpu.SemaphoreType.DMA((snaps - 1,)),
-            pltpu.SemaphoreType.DMA((snaps - 1,)),
-            pltpu.SemaphoreType.DMA((near,)),
-            pltpu.SemaphoreType.DMA((near,)),
-            pltpu.SemaphoreType.DMA((far,)),
-            pltpu.SemaphoreType.DMA((far,)),
+            pltpu.SemaphoreType.DMA,
+            pltpu.SemaphoreType.DMA,
+            pltpu.SemaphoreType.DMA,
+            pltpu.SemaphoreType.DMA,
+            pltpu.SemaphoreType.DMA,
+            pltpu.SemaphoreType.DMA,
+            pltpu.SemaphoreType.DMA,
         ],
         compiler_params=pltpu.CompilerParams(collective_id=0, has_side_effects=True),
     )(vel, ids, ref_order)
+    coherence = pltpu.with_memory_space_constraint(coherence, pltpu.VMEM)
+    spectrum = pltpu.with_memory_space_constraint(spectrum, pltpu.VMEM)
+    return pl.pallas_call(
+        put,
+        out_shape=(
+            jax.ShapeDtypeStruct((1, snaps, SHELLS), jnp.float32),
+            jax.ShapeDtypeStruct((1, SHELLS), jnp.float32),
+        ),
+        in_specs=[pl.BlockSpec(memory_space=pltpu.VMEM)] * 2,
+        out_specs=(pl.BlockSpec(memory_space=pl.ANY),) * 2,
+        scratch_shapes=[pltpu.SemaphoreType.DMA((2,))],
+    )(coherence, spectrum)
 
 
 def solution(mesh):

time: 19.1 us -> 18.4 us (0.963)
  local copies, waits for them, and re-layouts: 1.09 us -> 0 us
  Pallas kernels: 17.3 us -> 17.6 us
    unnamed x2 -> x0, local copies, waits for them, and re-layouts: 1.09 us -> none
    pallas_call x0 -> x1, Pallas kernels: none -> 0.6 us  [body(): pl.pallas_call(put, out_shape=(jax.ShapeDtypeStruct((1, snaps, SHELLS), j...]
    pallas_call x1, Pallas kernels: 17.3 us -> 17 us  [body(): pl.pallas_call(functools.partial(kernel, snaps, slabs, rows), out_shape=(...]
where the time goes in v3:
time: 18.4 us; the launch traced here: 18.2 us
  Pallas kernels  17.6 us (96%)
  between operations  0.64 us (3%)
    pallas_call x1, Pallas kernels, body(): pl.pallas_call(functools.partial(kernel, snaps, slabs, rows), out_shape=(...  17 us
    pallas_call x1, Pallas kernels, body(): pl.pallas_call(put, out_shape=(jax.ShapeDtypeStruct((1, snaps, SHELLS), j...  0.6 us

profile of v3, /device:TPU:0, one launch (start us, length us, event | category | flops | bytes accessed | tf_op | source)
XLA Modules:
  0.0 18.2 jit_solution(12161310935998976241)
XLA Ops:
  0.6 17.0 %shard_map.50 = (f32[1,4,128]{2,1,0:T(4,128)S(1)}, f32[1,128]{1,0:T(1,128)S(1)}) custom-call(bf16[3,256,128]{2,1,0:T(8,128)(2,1)} %bitcast.6, s32[128,128]{1,0:T(8,128)} %bitcast.7, s32[4]{0:T(128)} %order_ref.1), custom_call_target="tpu_custom_call" | custom-call | tf_op jit(solution)/shard_map/pallas_call | solution.py:206
  17.6 0.6 %shard_map.51 = (f32[1,4,128]{2,1,0:T(4,128)}, f32[1,128]{1,0:T(1,128)}) custom-call(f32[1,4,128]{2,1,0:T(4,128)S(1)} %get-tuple-element.4.coh_ref, f32[1,128]{1,0:T(1,128)S(1)} %get-tuple-element.5.spec_ref), custom_call_target="tpu_custom_call" | custom-call | tf_op jit(solution)/shard_map/pallas_call | solution.py:250
